TPU v7x, 128 devices: a whole 4x4x4 slice. The times are simulated.
128 devices in a mesh: gx: 16 (over y, z_lo, core), gy: 8 (over z_hi, x).
Axes of the slice: x: 4, y: 4, z: 4 (z_hi: 2, z_lo: 2; z = z_hi * 2 + z_lo), core: 2. Of those that a mesh axis runs over, the one named last changes fastest.
Arguments:
- kernels: bfloat16 [4, 4, 1024, 512, 128], P(None, None, 'gx', 'gy'), may hold values from -600 to 600
- event_weight: float32 [4], replicated, may hold values from 0.3 to 3
Outputs:
- smoothed: float32 [4, 1024, 512, 128], P(None, 'gx', 'gy')
All inputs are finite; a program needn't handle non-finite values.
Results may differ from a plain program's by a relative error of at most 0.0053.
Values may be sent and summed in bfloat16 or wider, within the bound.
No kernel may reach another device: no remote copies, remote signals or barrier semaphores. Data moves between devices by JAX's collectives and lax.ppermute only.
A program may use at most 192 MiB of HBM per device.

v0:
```python
import jax
import jax.numpy as jnp
from jax import lax
from jax.sharding import PartitionSpec as P

REACH = 3


def in_blocks(shard, dim, peers):
    before, after = (shard.shape[:dim], shard.shape[dim + 1 :])
    return jnp.moveaxis(shard.reshape(*before, peers, -1, *after), dim, 0)


def cut_rows(length, count):
    unit = 8 if length >= 8 * count else 1
    return [length // unit * k // count * unit for k in range(1, count)]


def joined_along(blocks, dim):
    dims = list(blocks.shape[1:])
    dims[dim] *= blocks.shape[0]
    return jnp.moveaxis(blocks, 0, dim).reshape(dims)


def several_exchanges(shard, axis, pieces, split_dim, concat_dim):
    blocks = in_blocks(shard, split_dim, lax.axis_size(axis))
    split_at = max(range(1, max(2, blocks.ndim - 1)), key=lambda d: blocks.shape[d])
    gathered = []
    for share in jnp.split(blocks, cut_rows(blocks.shape[split_at], pieces), axis=split_at):
        if share.size:
            gathered.append(lax.all_to_all(share, axis, split_axis=0, concat_axis=0, tiled=True))
    return joined_along(jnp.concatenate(gathered, axis=split_at), concat_dim)


def gauss_weights(offsets, radius, sigma):
    values = offsets.astype(jnp.float32)
    weights = jnp.exp(-values * values / (2.0 * sigma * sigma))
    return jnp.where(jnp.abs(offsets) <= radius, weights, 0.0).astype(jnp.bfloat16)


def apply_band(padded, dim, rows, total, radius, sigma):
    width = padded.shape[dim]
    shift = (width - rows) // 2
    row_ids = jnp.arange(rows, dtype=jnp.int32)
    col_ids = jnp.arange(width, dtype=jnp.int32)
    matrix = gauss_weights(col_ids[None, :] - row_ids[:, None] - shift, radius, sigma)
    if dim == 1:
        product = jnp.einsum("ij,pjyz->piyz", matrix, padded, preferred_element_type=jnp.float32)
    else:
        product = jnp.einsum("ij,pxjz->pxiz", matrix, padded, preferred_element_type=jnp.float32)
    steps = jnp.arange(-radius, radius + 1, dtype=jnp.int32)
    inside = (row_ids[:, None] + steps[None, :] >= 0) & (row_ids[:, None] + steps[None, :] < total)
    table = gauss_weights(steps, radius, sigma).astype(jnp.float32)
    norms = jnp.sum(jnp.where(inside, table[None, :], 0.0), axis=1)
    if dim == 1:
        return product / norms[None, :, None, None]
    return product / norms[None, None, :, None]


def body(kernels, event_weight):
    block = kernels.shape[2]
    radius = REACH * block
    sigma = 2.0 * block
    summed = jnp.sum(
        event_weight[:, None, None, None, None] * kernels.astype(jnp.float32), axis=0
    ).astype(jnp.bfloat16)
    lines = lax.all_to_all(summed, "gx", split_axis=2, concat_axis=1, tiled=True)
    total = lines.shape[1]
    done = apply_band(lines, 1, total, total, radius, sigma).astype(jnp.bfloat16)
    along_x = lax.all_to_all(done, "gx", split_axis=1, concat_axis=2, tiled=True)
    lines_y = several_exchanges(along_x, "gy", 2, 1, 2)
    total_y = lines_y.shape[2]
    done_y = apply_band(lines_y, 2, total_y, total_y, radius, sigma)
    result = lax.all_to_all(
        done_y.astype(jnp.bfloat16), "gy", split_axis=2, concat_axis=1, tiled=True
    ).astype(done_y.dtype)
    return result


def solution(mesh):
    return jax.shard_map(
        body,
        mesh=mesh,
        in_specs=(P(None, None, "gx", "gy", None), P()),
        out_specs=P(None, "gx", "gy", None),
        check_vma=False,
    )
```

profile of v0, /device:TPU:1, one launch (start us, length us, event | category | flops | bytes accessed | tf_op | source)
XLA Modules:
  0.0 310.5 jit_solution(15128894257158790863)
XLA Ops:
  0.0 13.7 %multiply_reduce_fusion = bf16[4,64,64,128]{3,2,1,0:T(8,128)(2,1)S(1)} fusion(bf16[4,4,64,64,128]{4,3,2,1,0:T(8,128)(2,1)} %param.2, f32[4]{0:T(128)} %param.3), kind=kLoop, calls=%fused_computation | loop fusion | flops 23068672 | bytes 20971536 | tf_op jit(solution)/shard_map/reduce_sum | solution.py:64
  13.7 4.7 %copy.34 = bf16[4,64,64,128]{3,1,0,2:T(8,128)(2,1)} copy(bf16[4,64,64,128]{3,2,1,0:T(8,128)(2,1)S(1)} %multiply_reduce_fusion) | data formatting | bytes 8388608 | tf_op jit(solution)/shard_map/convert_element_type | solution.py:66
  18.4 7.3 %all-to-all-start = ((bf16[4,64,64,128]{3,1,0,2:T(8,128)(2,1)}), bf16[4,64,64,128]{3,1,0,2:T(8,128)(2,1)}, u32[]{:S(2)}, u32[]{:S(2)}) async-start(bf16[4,64,64,128]{3,1,0,2:T(8,128)(2,1)} %copy.34), calls=%async_computation | async-start | bytes 8388608 | tf_op jit(solution)/shard_map/all_to_all | solution.py:67
  26.2 52.7 %all-to-all-done = bf16[4,64,64,128]{3,1,0,2:T(8,128)(2,1)} async-done(((bf16[4,64,64,128]{3,1,0,2:T(8,128)(2,1)}), bf16[4,64,64,128]{3,1,0,2:T(8,128)(2,1)}, u32[]{:S(2)}, u32[]{:S(2)}) %all-to-all-start) | async-done | bytes 4194336 | tf_op jit(solution)/shard_map/all_to_all | solution.py:67
  78.9 3.1 %copy.36 = bf16[4,16,64,4,128]{4,2,1,3,0:T(8,128)(2,1)S(1)} copy(bf16[4,16,64,4,128]{4,2,0,3,1:T(8,128)(2,1)} %bitcast.2) | data formatting | bytes 8388608 | tf_op jit(solution)/shard_map/all_to_all | solution.py:67
  82.0 6.5 %fusion.4 = bf16[4,1024,4,128]{1,3,2,0:T(8,128)(2,1)} fusion(f32[1024]{0:T(1024)S(1)} %select_reduce_fusion, bf16[4,1024,4,128]{3,1,2,0:T(8,128)(2,1)S(1)} %bitcast.38), kind=kOutput, calls=%fused_computation.11 | convolution fusion | flops 4308598784 | bytes 8392704 | tf_op jit(solution)/shard_map/ij,pjyz->piyz/dot_general | solution.py:48
  88.5 7.8 %copy.38 = bf16[4,1024,4,128]{3,2,0,1:T(4,128)(2,1)} copy(bf16[4,1024,4,128]{1,3,2,0:T(8,128)(2,1)} %fusion.4) | data formatting | bytes 8388608 | tf_op jit(solution)/shard_map/convert_element_type | solution.py:69
  96.4 60.8 %all_to_all.52 = bf16[4,1024,4,128]{3,2,0,1:T(4,128)(2,1)S(1)} all-to-all(bf16[4,1024,4,128]{3,2,0,1:T(4,128)(2,1)} %copy.38), channel_id=1, replica_groups=mesh['gx'=16,'gy'=8] {'gx'}, dimensions={1} | all-to-all | bytes 8388608 | tf_op jit(solution)/shard_map/all_to_all | solution.py:70
  158.3 1.4 copy.40
  159.7 2.3 fusion.37
  162.0 1.9 copy.41
  163.9 7.0 %all-to-all-start.2 = ((bf16[8,4,8,32,128]{4,2,3,1,0:T(8,128)(2,1)}), bf16[8,4,8,32,128]{4,2,3,1,0:T(8,128)(2,1)S(1)}, u32[]{:S(2)}, u32[]{:S(2)}) async-start(bf16[8,4,8,32,128]{4,2,3,1,0:T(8,128)(2,1)} %copy.41), calls=%async_computation.2 | async-start | bytes 4194304 | tf_op jit(solution)/shard_map/all_to_all | solution.py:31
  170.9 3.5 %copy.42 = bf16[8,4,8,32,128]{4,2,3,1,0:T(8,128)(2,1)} copy(bf16[8,4,8,32,128]{4,2,0,3,1:T(8,128)(2,1)} %get-tuple-element.6) | data formatting | bytes 4194304 | tf_op jit(solution)/shard_map/split | solution.py:29
  174.4 25.1 %all-to-all-done.2 = bf16[8,4,8,32,128]{4,2,3,1,0:T(8,128)(2,1)S(1)} async-done(((bf16[8,4,8,32,128]{4,2,3,1,0:T(8,128)(2,1)}), bf16[8,4,8,32,128]{4,2,3,1,0:T(8,128)(2,1)S(1)}, u32[]{:S(2)}, u32[]{:S(2)}) %all-to-all-start.2) | async-done | bytes 2097184 | tf_op jit(solution)/shard_map/all_to_all | solution.py:31
  199.5 4.4 %all-to-all-start.3 = ((bf16[8,4,8,32,128]{4,2,3,1,0:T(8,128)(2,1)}), bf16[8,4,8,32,128]{4,2,3,1,0:T(8,128)(2,1)}, u32[]{:S(2)}, u32[]{:S(2)}) async-start(bf16[8,4,8,32,128]{4,2,3,1,0:T(8,128)(2,1)} %copy.42), calls=%async_computation.3 | async-start | bytes 4194304 | tf_op jit(solution)/shard_map/all_to_all | solution.py:31
  204.1 1.8 copy.43
  205.9 26.6 %all-to-all-done.3 = bf16[8,4,8,32,128]{4,2,3,1,0:T(8,128)(2,1)} async-done(((bf16[8,4,8,32,128]{4,2,3,1,0:T(8,128)(2,1)}), bf16[8,4,8,32,128]{4,2,3,1,0:T(8,128)(2,1)}, u32[]{:S(2)}, u32[]{:S(2)}) %all-to-all-start.3) | async-done | bytes 2097184 | tf_op jit(solution)/shard_map/all_to_all | solution.py:31
  232.5 2.1 copy.44
  234.6 1.3 pad_maximum_fusion
  235.9 4.5 %fusion.5 = bf16[4,8,512,128]{2,3,1,0:T(8,128)(2,1)} fusion(f32[512]{0:T(512)S(1)} %select_reduce_fusion.1, bf16[4,8,512,128]{3,2,1,0:T(8,128)(2,1)S(1)} %bitcast.37), kind=kOutput, calls=%fused_computation.12 | convolution fusion | flops 2154037248 | bytes 8390656 | tf_op jit(solution)/shard_map/ij,pxjz->pxiz/dot_general | solution.py:50
  240.4 7.9 %copy.46 = bf16[4,8,512,128]{3,1,0,2:T(8,128)(2,1)} copy(bf16[4,8,512,128]{2,3,1,0:T(8,128)(2,1)} %fusion.5) | data formatting | bytes 8388608 | tf_op jit(solution)/shard_map/convert_element_type | solution.py:75
  248.3 55.3 %all_to_all.53 = bf16[4,8,512,128]{3,1,0,2:T(8,128)(2,1)S(1)} all-to-all(bf16[4,8,512,128]{3,1,0,2:T(8,128)(2,1)} %copy.46), channel_id=1, replica_groups=mesh['gx'=16,'gy'=8] {'gy'}, dimensions={2} | all-to-all | bytes 8388608 | tf_op jit(solution)/shard_map/all_to_all | solution.py:74
  303.5 1.6 copy.47
  306.2 4.2 %copy.48 = f32[4,8,8,64,128]{4,3,2,1,0:T(8,128)} copy(f32[4,8,8,64,128]{4,3,1,2,0:T(8,128)S(1)} %convert_bitcast_fusion) | data formatting | bytes 16777216 | tf_op jit(solution)/shard_map/convert_element_type | solution.py:76
  (8 shorter events, 2.8 us)
Async XLA Ops:
  18.4 60.4 %all-to-all-start = ((bf16[4,64,64,128]{3,1,0,2:T(8,128)(2,1)}), bf16[4,64,64,128]{3,1,0,2:T(8,128)(2,1)}, u32[]{:S(2)}, u32[]{:S(2)}) async-start(bf16[4,64,64,128]{3,1,0,2:T(8,128)(2,1)} %copy.34), calls=%async_computation | async-start | bytes 8388608 | tf_op jit(solution)/shard_map/all_to_all | solution.py:67
  163.9 35.6 %all-to-all-start.2 = ((bf16[8,4,8,32,128]{4,2,3,1,0:T(8,128)(2,1)}), bf16[8,4,8,32,128]{4,2,3,1,0:T(8,128)(2,1)S(1)}, u32[]{:S(2)}, u32[]{:S(2)}) async-start(bf16[8,4,8,32,128]{4,2,3,1,0:T(8,128)(2,1)} %copy.41), calls=%async_computation.2 | async-start | bytes 4194304 | tf_op jit(solution)/shard_map/all_to_all | solution.py:31
  199.5 33.0 %all-to-all-start.3 = ((bf16[8,4,8,32,128]{4,2,3,1,0:T(8,128)(2,1)}), bf16[8,4,8,32,128]{4,2,3,1,0:T(8,128)(2,1)}, u32[]{:S(2)}, u32[]{:S(2)}) async-start(bf16[8,4,8,32,128]{4,2,3,1,0:T(8,128)(2,1)} %copy.42), calls=%async_computation.3 | async-start | bytes 4194304 | tf_op jit(solution)/shard_map/all_to_all | solution.py:31
  205.9 28.7 %copy-start = (bf16[8,4,8,32,128]{4,3,0,2,1:T(8,128)(2,1)S(1)}, bf16[8,4,8,32,128]{4,3,0,2,1:T(8,128)(2,1)}, u32[]{:S(2)}) copy-start(bf16[8,4,8,32,128]{4,3,0,2,1:T(8,128)(2,1)} %copy.43) | copy-start | bytes 6291460
where the time goes:
time: 312 us; the launch traced here: 310 us
  blocking collectives  116 us (37%)
  waiting for transfers between devices  104 us (33%)
  local copies, waits for them, and re-layouts  43.5 us (14%)
  starting transfers between devices  18.7 us (6%)
  other arithmetic  16.7 us (5%)
  matrix products  11 us (4%)
    all_to_all x1, blocking collectives, body(): lax.all_to_all(done, 'gx', split_axis=1, concat_axis=2, tiled=True)  60.8 us
    all_to_all x1, blocking collectives, body(): lax.all_to_all(done_y.astype(jnp.bfloat16), 'gy', split_axis=2, concat_ax...  55.3 us
    all_to_all x1, waiting for transfers between devices, body(): lax.all_to_all(summed, 'gx', split_axis=2, concat_axis=1, tiled=True)  52.7 us
    all_to_all x2, waiting for transfers between devices, several_exchanges(): lax.all_to_all(share, axis, split_axis=0, concat_axis=0, tiled=True)  51.7 us
    reduce_sum x1, other arithmetic, body(): jnp.sum(event_weight[:, None, None, None, None] * kernels.astype(jnp.floa...  13.7 us
    all_to_all x2, starting transfers between devices, several_exchanges(): lax.all_to_all(share, axis, split_axis=0, concat_axis=0, tiled=True)  11.4 us
    convert_element_type x1, local copies, waits for them, and re-layouts, body(): done_y.astype(jnp.bfloat16)  7.9 us
    convert_element_type x1, local copies, waits for them, and re-layouts, body(): apply_band(lines, 1, total, total, radius, sigma).astype(jnp.bfloat16)  7.84 us
  transfers between devices with their start and end apart: 3, of which 3 were waited for; matrix products, arithmetic and copies ran while one was open for 2% of the time, Pallas kernels for 0%

commit v1 on v0

v1 whole, which is shorter than its diff:
```python
import functools
import jax
import jax.numpy as jnp
from jax import lax
from jax.experimental import pallas as pl
from jax.experimental.pallas import tpu as pltpu
from jax.sharding import PartitionSpec as P

REACH = 3
AXES = ("gx", "gy")
ROWS = 8


def gauss_weights(offsets, radius, sigma):
    values = offsets.astype(jnp.float32)
    weights = jnp.exp(-values * values / (2.0 * sigma * sigma))
    return jnp.where(jnp.abs(offsets) <= radius, weights, 0.0).astype(jnp.bfloat16)


def inverse_norms(total, radius, sigma):
    steps = jnp.arange(-radius, radius + 1, dtype=jnp.int32)
    places = jnp.arange(total, dtype=jnp.int32)[:, None] + steps[None, :]
    table = gauss_weights(steps, radius, sigma).astype(jnp.float32)
    inside = (places >= 0) & (places < total)
    return 1.0 / jnp.sum(jnp.where(inside, table[None, :], 0.0), axis=1)


def sum_kernel(weight_ref, kernels_ref, out_ref, turned):
    events, _, halves, rows, width, depth = kernels_ref.shape
    for r in range(rows):
        parts = []
        for h in range(halves):
            total = weight_ref[0] * kernels_ref[0, 0, h, r].astype(jnp.float32)
            for e in range(1, events):
                total = total + weight_ref[e] * kernels_ref[e, 0, h, r].astype(jnp.float32)
            parts.append(total)
        turned[pl.ds(r, depth, stride=rows), :] = jnp.concatenate(parts, axis=0).T
    out_ref[:, 0] = turned[...].reshape(depth, rows, halves * width).astype(out_ref.dtype)


def event_sum(kernels, event_weight):
    events, params, nx, ny, depth = kernels.shape
    halves = depth // ny
    split = kernels.reshape(events, params, halves, nx // halves, ny, depth)
    return pl.pallas_call(
        sum_kernel,
        grid=(params, nx // halves // ROWS),
        in_specs=[
            pl.BlockSpec(memory_space=pltpu.SMEM),
            pl.BlockSpec((events, 1, halves, ROWS, ny, depth), lambda p, r: (0, p, 0, r, 0, 0)),
        ],
        out_specs=pl.BlockSpec((depth, 1, ROWS, halves * ny), lambda p, r: (0, p, r, 0)),
        out_shape=jax.ShapeDtypeStruct((depth, params, nx // halves, halves * ny), jnp.bfloat16),
        scratch_shapes=[pltpu.VMEM((depth * ROWS, halves * ny), jnp.float32)],
        name="event_sum",
    )(event_weight, split)


def smooth_kernel(size_y, block, in_ref, tile_ref, tile_t_ref, inv_x_ref, inv_y_ref, out_ref, plane):
    nx, ny = plane.shape
    rows = in_ref.shape[2]
    tile, reach = tile_ref.shape[0], REACH * block
    pair = 2 * block

    @pl.loop(0, nx // block)
    def _(i):
        for j in range(0, size_y, 2):
            a, b = in_ref[i * size_y + j, 0], in_ref[i * size_y + j + 1, 0]
            cols = pl.ds(j * block, pair)
            plane[pl.ds(i * block, rows), cols] = jnp.concatenate([a[:, :block], b[:, :block]], axis=1)
            plane[pl.ds(i * block + rows, rows), cols] = jnp.concatenate([a[:, block:], b[:, block:]], axis=1)

    for x0 in range(0, nx, tile):
        lo, hi = max(0, x0 - reach), min(nx, x0 + tile + reach)
        at = lo - (x0 - reach)
        sums = jnp.dot(tile_ref[:, at : at + hi - lo], plane[lo:hi], preferred_element_type=jnp.float32)
        along_x = (sums * inv_x_ref[x0 : x0 + tile]).astype(jnp.bfloat16)
        for y0 in range(0, ny, tile):
            lo, hi = max(0, y0 - reach), min(ny, y0 + tile + reach)
            at = lo - (y0 - reach)
            sums = jnp.dot(along_x[:, lo:hi], tile_t_ref[at : at + hi - lo], preferred_element_type=jnp.float32)
            done = (sums * inv_y_ref[:, y0 : y0 + tile]).astype(jnp.bfloat16)
            for i in range(tile // block):
                for j in range(0, tile // block, 2):
                    part = done[i * block : (i + 1) * block, j * block : j * block + pair]
                    a, b = part[:rows], part[rows:]
                    at_block = (x0 // block + i) * size_y + y0 // block + j
                    out_ref[at_block, 0] = jnp.concatenate([a[:, :block], b[:, :block]], axis=1)
                    out_ref[at_block + 1, 0] = jnp.concatenate([a[:, block:], b[:, block:]], axis=1)


def smooth(lines, block, size_x, size_y, tables):
    blocks, params, rows, width = lines.shape
    nx, ny = size_x * block, size_y * block
    whole = lambda a: pl.BlockSpec(a.shape, lambda p: (0,) * a.ndim)
    spec = pl.BlockSpec((blocks, 1, rows, width), lambda p: (0, p, 0, 0))
    return pl.pallas_call(
        functools.partial(smooth_kernel, size_y, block),
        grid=(params,),
        in_specs=[spec] + [whole(t) for t in tables],
        out_specs=spec,
        out_shape=jax.ShapeDtypeStruct(lines.shape, jnp.bfloat16),
        scratch_shapes=[pltpu.VMEM((nx, ny), jnp.bfloat16)],
        name="smooth",
    )(lines, *tables)


def turn_kernel(in_ref, out_ref, wide):
    depth, _, rows, pair = in_ref.shape
    halves, width = out_ref.shape[1], out_ref.shape[3]
    wide[...] = in_ref[:, 0].astype(jnp.float32).reshape(depth * rows, pair)
    for r in range(rows):
        turned = wide[pl.ds(r, depth, stride=rows), :].T
        for h in range(halves):
            out_ref[0, h, r] = turned[h * width : (h + 1) * width]


def turn_back(done, block):
    depth, params, rows, pair = done.shape
    halves = pair // block
    out = pl.pallas_call(
        turn_kernel,
        grid=(params, rows // ROWS),
        in_specs=[pl.BlockSpec((depth, 1, ROWS, pair), lambda p, r: (0, p, r, 0))],
        out_specs=pl.BlockSpec((1, halves, ROWS, block, depth), lambda p, r: (p, 0, r, 0, 0)),
        out_shape=jax.ShapeDtypeStruct((params, halves, rows, block, depth), jnp.float32),
        scratch_shapes=[pltpu.VMEM((depth * ROWS, pair), jnp.float32)],
        name="turn_back",
    )(done)
    return out.reshape(params, halves * rows, block, depth)


def body(kernels, event_weight):
    block = kernels.shape[2]
    radius, sigma = REACH * block, 2.0 * block
    size_x, size_y = lax.axis_size("gx"), lax.axis_size("gy")
    tile = 4 * block
    offsets = jnp.arange(tile + 2 * radius)[None, :] - jnp.arange(tile)[:, None] - radius
    tables = (
        gauss_weights(offsets, radius, sigma),
        gauss_weights(offsets.T, radius, sigma),
        inverse_norms(size_x * block, radius, sigma)[:, None],
        inverse_norms(size_y * block, radius, sigma)[None, :],
    )
    summed = event_sum(kernels, event_weight)
    planes = lax.all_to_all(summed, AXES, split_axis=0, concat_axis=0, tiled=True)
    done = smooth(planes, block, size_x, size_y, tables)
    blocks = lax.all_to_all(done, AXES, split_axis=0, concat_axis=0, tiled=True)
    return turn_back(blocks, block)


def solution(mesh):
    return jax.shard_map(
        body,
        mesh=mesh,
        in_specs=(P(None, None, "gx", "gy", None), P()),
        out_specs=P(None, "gx", "gy", None),
        check_vma=False,
    )
```

time: 312 us -> 169 us (0.54)
  blocking collectives: 116 us -> 58.8 us
  waiting for transfers between devices: 104 us -> 48.7 us
  Pallas kernels: 0 us -> 44 us
  local copies, waits for them, and re-layouts: 43.5 us -> 1.03 us
  other arithmetic: 16.7 us -> 3.2 us
  matrix products: 11 us -> 0 us
  starting transfers between devices: 18.7 us -> 11.9 us
    all_to_all x2 -> x1, blocking collectives: 116 us -> 58.8 us  [body(): blocks = lax.all_to_all(done, AXES, split_axis=0, concat_axis=0, tiled=True)]
    all_to_all x3 -> x1, waiting for transfers between devices: 104 us -> 48.7 us  [body(): lax.all_to_all(summed, AXES, split_axis=0, concat_axis=0, tiled=True)]
    pallas_call x0 -> x3, Pallas kernels: none -> 44 us  [the longest x1 17 us: smooth(): pl.pallas_call(functools.partial(smooth_kernel, size_y, block), grid=(par...]
    convert_element_type x4 -> x0, local copies, waits for them, and re-layouts: 24.7 us -> none  [the longest x1 7.9 us: body(): done_y.astype(jnp.bfloat16)]
    reduce_sum x3 -> x2, other arithmetic: 14.3 us -> 0.62 us  [inverse_norms(): return 1.0 / jnp.sum(jnp.where(inside, table[None, :], 0.0), axis=1)]
    all_to_all x6 -> x0, local copies, waits for them, and re-layouts: 11.1 us -> none  [the longest x2 3.86 us: several_exchanges(): lax.all_to_all(share, axis, split_axis=0, concat_axis=0, tiled=True)]
    dot_general x2 -> x0, matrix products: 11 us -> none  [the longest x1 6.52 us: apply_band(): jnp.einsum('ij,pjyz->piyz', matrix, padded, preferred_element_type=jnp.fl...]
    split x3 -> x0, local copies, waits for them, and re-layouts: 7.67 us -> none  [several_exchanges(): jnp.split(blocks, cut_rows(blocks.shape[split_at], pieces), axis=split_at)]
  transfers between devices with their start and end apart: 3 -> 1, of which waited for: 3 -> 1; matrix products, arithmetic and copies ran while one was open for 2% -> 3% of each run, Pallas kernels for 0% -> 0%
where the time goes in v1:
time: 169 us; the launch traced here: 168 us
  blocking collectives  58.8 us (35%)
  waiting for transfers between devices  48.7 us (29%)
  Pallas kernels  44 us (26%)
  starting transfers between devices  11.9 us (7%)
  other arithmetic  3.2 us (2%)
    all_to_all x1, blocking collectives, body(): blocks = lax.all_to_all(done, AXES, split_axis=0, concat_axis=0, tiled=True)  58.8 us
    all_to_all x1, waiting for transfers between devices, body(): lax.all_to_all(summed, AXES, split_axis=0, concat_axis=0, tiled=True)  48.7 us
    pallas_call x1, Pallas kernels, smooth(): pl.pallas_call(functools.partial(smooth_kernel, size_y, block), grid=(par...  17 us
    pallas_call x1, Pallas kernels, event_sum(): pl.pallas_call(sum_kernel, grid=(params, nx // halves // ROWS), in_specs=...  14.7 us
    pallas_call x1, Pallas kernels, turn_back(): pl.pallas_call(turn_kernel, grid=(params, rows // ROWS), in_specs=[pl.Blo...  12.3 us
    all_to_all x1, starting transfers between devices, body(): lax.all_to_all(summed, AXES, split_axis=0, concat_axis=0, tiled=True)  11.9 us
  transfers between devices with their start and end apart: 1, of which 1 were waited for; matrix products, arithmetic and copies ran while one was open for 3% of the time, Pallas kernels for 0%

profile of v1, /device:TPU:1, one launch (start us, length us, event | category | flops | bytes accessed | tf_op | source)
XLA Modules:
  0.0 167.8 jit_solution(2578689969523242135)
XLA Ops:
  0.0 14.7 %event_sum.1 = bf16[128,4,32,128]{3,2,1,0:T(8,128)(2,1)} custom-call(f32[4]{0:T(128)} %weight_ref.1, bf16[4,4,2,32,64,128]{5,4,3,2,1,0:T(8,128)(2,1)} %bitcast.4), custom_call_target="tpu_custom_call" | custom-call | tf_op jit(solution)/shard_map/event_sum/pallas_call | solution.py:45
  14.7 11.9 %all-to-all-start = ((bf16[128,4,32,128]{3,2,1,0:T(8,128)(2,1)}), bf16[128,4,32,128]{3,2,1,0:T(8,128)(2,1)}, u32[]{:S(2)}, u32[]{:S(2)}) async-start(bf16[128,4,32,128]{3,2,1,0:T(8,128)(2,1)} %event_sum.1), calls=%async_computation | async-start | bytes 8388608 | tf_op jit(solution)/shard_map/all_to_all | solution.py:146
  26.7 0.4 select_reduce_fusion
  27.1 1.0 copy.4.inv_x_ref
  28.1 1.0 fusion.13.tile_t_ref
  29.1 1.0 fusion.9.tile_ref
  30.1 0.2 select_reduce_fusion.1
  30.3 0.6 broadcast_divide_fusion.1
  30.9 48.7 %all-to-all-done.in_ref = bf16[128,4,32,128]{3,2,1,0:T(8,128)(2,1)} async-done(((bf16[128,4,32,128]{3,2,1,0:T(8,128)(2,1)}), bf16[128,4,32,128]{3,2,1,0:T(8,128)(2,1)}, u32[]{:S(2)}, u32[]{:S(2)}) %all-to-all-start) | async-done | bytes 4194336 | tf_op jit(solution)/shard_map/all_to_all | solution.py:146
  79.7 17.0 %smooth.1 = bf16[128,4,32,128]{3,2,1,0:T(8,128)(2,1)} custom-call(bf16[128,4,32,128]{3,2,1,0:T(8,128)(2,1)} %all-to-all-done.in_ref, bf16[256,640]{1,0:T(8,128)(2,1)} %fusion.9.tile_ref, bf16[640,256]{1,0:T(8,128)(2,1)} %fusion.13.tile_t_ref, f32[1024,1]{1,0:T(8,128)} %copy.4.inv_x_ref, f32[1,512]{1,0:T(1,128)} %bitcast.6), custom_call_target="tpu_custom_call" | custom-call | tf_op jit(solution)/shard_map/smooth/pallas_call | solution.py:97
  96.6 58.8 %all_to_all.10.in_ref = bf16[128,4,32,128]{3,2,1,0:T(8,128)(2,1)} all-to-all(bf16[128,4,32,128]{3,2,1,0:T(8,128)(2,1)} %smooth.1), channel_id=1, replica_groups=mesh['gx'=16,'gy'=8] {'gx','gy'}, dimensions={0} | all-to-all | bytes 8388608 | tf_op jit(solution)/shard_map/all_to_all | solution.py:148
  155.5 12.3 %turn_back.1 = f32[4,2,32,64,128]{4,3,2,1,0:T(8,128)} custom-call(bf16[128,4,32,128]{3,2,1,0:T(8,128)(2,1)} %all_to_all.10.in_ref), custom_call_target="tpu_custom_call" | custom-call | tf_op jit(solution)/shard_map/turn_back/pallas_call | solution.py:121
  (3 shorter events, 0.0 us)
Async XLA Ops:
  14.7 64.9 %all-to-all-start = ((bf16[128,4,32,128]{3,2,1,0:T(8,128)(2,1)}), bf16[128,4,32,128]{3,2,1,0:T(8,128)(2,1)}, u32[]{:S(2)}, u32[]{:S(2)}) async-start(bf16[128,4,32,128]{3,2,1,0:T(8,128)(2,1)} %event_sum.1), calls=%async_computation | async-start | bytes 8388608 | tf_op jit(solution)/shard_map/all_to_all | solution.py:146

commit v2 on v1

v2 whole, which is shorter than its diff:
```python
import functools
import jax
import jax.numpy as jnp
from jax import lax
from jax.experimental import pallas as pl
from jax.experimental.pallas import tpu as pltpu
from jax.sharding import PartitionSpec as P

REACH = 3
AXES = ("gx", "gy")
TILE = 4
SUM_MIB = 36
ROWS = 8


def gauss_weights(offsets, radius, sigma):
    values = offsets.astype(jnp.float32)
    weights = jnp.exp(-values * values / (2.0 * sigma * sigma))
    return jnp.where(jnp.abs(offsets) <= radius, weights, 0.0).astype(jnp.bfloat16)


def band(rows, cols, shift, axis, sigma, radius):
    far = lax.broadcasted_iota(jnp.int32, (rows, cols), axis)
    near = lax.broadcasted_iota(jnp.int32, (rows, cols), 1 - axis)
    return gauss_weights(far - near - shift, radius, sigma)


def sum_kernel(block, weight_ref, kernels_ref, out_ref, tile_ref, tile_t_ref, inv_x_ref, inv_y_ref, landing, turned, arrived):
    steps, events, halves, rows, width, depth = landing.shape
    per_param = steps // kernels_ref.shape[1]
    radius, sigma = REACH * block, 2.0 * block

    def copy(s):
        p, r = s // per_param, lax.rem(s, per_param)
        return pltpu.make_async_copy(
            kernels_ref.at[:, p, :, pl.ds(r * rows, rows)], landing.at[s], arrived.at[s]
        )

    @pl.loop(0, steps)
    def _(s):
        copy(s).start()

    tile, reach = tile_ref.shape
    weights = band(tile, reach, radius, 1, sigma, radius)
    tile_ref[...] = weights
    weights_t = band(reach, tile, radius, 0, sigma, radius)
    tile_t_ref[...] = weights_t
    nx, ny = inv_x_ref.shape[0], inv_y_ref.shape[1]
    for x0 in range(0, nx, tile):
        lo, hi = clipped(x0, tile, radius, nx)
        sums = jnp.sum(weights[:, lo:hi].astype(jnp.float32), axis=1, keepdims=True)
        inv_x_ref[x0 : x0 + tile] = jnp.broadcast_to(1.0 / sums, (tile, inv_x_ref.shape[1]))
    for y0 in range(0, ny, tile):
        lo, hi = clipped(y0, tile, radius, ny)
        sums = jnp.sum(weights_t[lo:hi].astype(jnp.float32), axis=0, keepdims=True)
        inv_y_ref[:, y0 : y0 + tile] = jnp.broadcast_to(1.0 / sums, (inv_y_ref.shape[0], tile))

    @pl.loop(0, steps)
    def _(s):
        copy(s).wait()
        for r in range(rows):
            parts = []
            for h in range(halves):
                total = weight_ref[0] * landing[s, 0, h, r].astype(jnp.float32)
                for e in range(1, events):
                    total = total + weight_ref[e] * landing[s, e, h, r].astype(jnp.float32)
                parts.append(total)
            turned[pl.ds(r, depth, stride=rows), :] = jnp.concatenate(parts, axis=0).T
        p, place = s // per_param, pl.multiple_of(lax.rem(s, per_param) * rows, rows)
        whole = turned[...].reshape(depth, rows, halves * width)
        out_ref[:, p, pl.ds(place, rows)] = whole.astype(out_ref.dtype)


def clipped(first, tile, radius, total):
    return max(0, radius - first), min(tile + 2 * radius, total - first + radius)


def event_sum(kernels, event_weight, nx_all, ny_all):
    events, params, nx, ny, depth = kernels.shape
    halves = depth // ny
    rows = nx // halves
    split = kernels.reshape(events, params, halves, rows, ny, depth)
    tile, reach = TILE * nx, (TILE + 2 * REACH) * nx
    steps = params * rows // ROWS
    vmem = pl.BlockSpec(memory_space=pltpu.VMEM)
    return pl.pallas_call(
        functools.partial(sum_kernel, nx),
        in_specs=[pl.BlockSpec(memory_space=pltpu.SMEM), pl.BlockSpec(memory_space=pl.ANY)],
        out_specs=(vmem,) * 5,
        out_shape=(
            jax.ShapeDtypeStruct((depth, params, rows, halves * ny), jnp.bfloat16),
            jax.ShapeDtypeStruct((tile, reach), jnp.bfloat16),
            jax.ShapeDtypeStruct((reach, tile), jnp.bfloat16),
            jax.ShapeDtypeStruct((nx_all, depth), jnp.float32),
            jax.ShapeDtypeStruct((8, ny_all), jnp.float32),
        ),
        scratch_shapes=[
            pltpu.VMEM((steps, events, halves, ROWS, ny, depth), jnp.bfloat16),
            pltpu.VMEM((depth * ROWS, halves * ny), jnp.float32),
            pltpu.SemaphoreType.DMA((steps,)),
        ],
        compiler_params=pltpu.CompilerParams(vmem_limit_bytes=SUM_MIB << 20),
        name="event_sum",
    )(event_weight, split)


def smooth_kernel(size_y, block, in_ref, tile_ref, tile_t_ref, inv_x_ref, inv_y_ref, out_ref, plane):
    nx, ny = plane.shape
    rows = in_ref.shape[2]
    tile, reach = tile_ref.shape[0], REACH * block
    pair = 2 * block

    def build(i):
        for j in range(0, size_y, 2):
            a, b = in_ref[i * size_y + j, 0], in_ref[i * size_y + j + 1, 0]
            cols = slice(j * block, j * block + pair)
            plane[i * block : i * block + rows, cols] = jnp.concatenate([a[:, :block], b[:, :block]], axis=1)
            plane[i * block + rows : (i + 1) * block, cols] = jnp.concatenate([a[:, block:], b[:, block:]], axis=1)

    built = 0
    for x0 in range(0, nx, tile):
        lo, hi = max(0, x0 - reach), min(nx, x0 + tile + reach)
        while built * block < hi:
            build(built)
            built += 1
        at = lo - (x0 - reach)
        sums = jnp.dot(tile_ref[:, at : at + hi - lo], plane[lo:hi], preferred_element_type=jnp.float32)
        inv_x = jnp.concatenate([inv_x_ref[x0 : x0 + tile]] * (ny // inv_x_ref.shape[1]), axis=1)
        along_x = (sums * inv_x).astype(jnp.bfloat16)
        for y0 in range(0, ny, tile):
            lo, hi = max(0, y0 - reach), min(ny, y0 + tile + reach)
            at = lo - (y0 - reach)
            sums = jnp.dot(along_x[:, lo:hi], tile_t_ref[at : at + hi - lo], preferred_element_type=jnp.float32)
            done = (sums * inv_y_ref[0:1, y0 : y0 + tile]).astype(jnp.bfloat16)
            for i in range(tile // block):
                for j in range(0, tile // block, 2):
                    part = done[i * block : (i + 1) * block, j * block : j * block + pair]
                    a, b = part[:rows], part[rows:]
                    at_block = (x0 // block + i) * size_y + y0 // block + j
                    out_ref[at_block, 0] = jnp.concatenate([a[:, :block], b[:, :block]], axis=1)
                    out_ref[at_block + 1, 0] = jnp.concatenate([a[:, block:], b[:, block:]], axis=1)


def smooth(lines, block, size_x, size_y, tables):
    blocks, params, rows, width = lines.shape
    nx, ny = size_x * block, size_y * block
    whole = lambda a: pl.BlockSpec(a.shape, lambda p: (0,) * a.ndim)
    spec = pl.BlockSpec((blocks, 1, rows, width), lambda p: (0, p, 0, 0))
    return pl.pallas_call(
        functools.partial(smooth_kernel, size_y, block),
        grid=(params,),
        in_specs=[spec] + [whole(t) for t in tables],
        out_specs=spec,
        out_shape=jax.ShapeDtypeStruct(lines.shape, jnp.bfloat16),
        scratch_shapes=[pltpu.VMEM((nx, ny), jnp.bfloat16)],
        compiler_params=pltpu.CompilerParams(vmem_limit_bytes=16 << 20),
        name="smooth",
    )(lines, *tables)


def turn_kernel(in_ref, out_ref, leaving, wide, left):
    steps, halves, rows, width, _ = leaving.shape
    depth, params, _, pair = in_ref.shape
    per_param = steps // params

    def copy(s):
        p, r = s // per_param, lax.rem(s, per_param)
        return pltpu.make_async_copy(leaving.at[s], out_ref.at[p, :, pl.ds(r * rows, rows)], left.at[s])

    @pl.loop(0, steps)
    def _(s):
        p, place = s // per_param, pl.multiple_of(lax.rem(s, per_param) * rows, rows)
        wide[...] = in_ref[:, p, pl.ds(place, rows)].astype(jnp.float32).reshape(depth * rows, pair)
        for r in range(rows):
            turned = wide[pl.ds(r, depth, stride=rows), :].T
            for h in range(halves):
                leaving[s, h, r] = turned[h * width : (h + 1) * width]
        copy(s).start()

    @pl.loop(0, steps)
    def _(s):
        copy(s).wait()


def turn_back(done, block):
    depth, params, rows, pair = done.shape
    halves = pair // block
    steps = params * rows // ROWS
    out = pl.pallas_call(
        turn_kernel,
        in_specs=[pl.BlockSpec(memory_space=pltpu.VMEM)],
        out_specs=pl.BlockSpec(memory_space=pl.ANY),
        out_shape=jax.ShapeDtypeStruct((params, halves, rows, block, depth), jnp.float32),
        scratch_shapes=[
            pltpu.VMEM((steps, halves, ROWS, block, depth), jnp.float32),
            pltpu.VMEM((depth * ROWS, pair), jnp.float32),
            pltpu.SemaphoreType.DMA((steps,)),
        ],
        compiler_params=pltpu.CompilerParams(vmem_limit_bytes=24 << 20),
        name="turn_back",
    )(done)
    return out.reshape(params, halves * rows, block, depth)


def body(kernels, event_weight):
    block = kernels.shape[2]
    size_x, size_y = lax.axis_size("gx"), lax.axis_size("gy")
    summed, *tables = event_sum(kernels, event_weight, size_x * block, size_y * block)
    swap = functools.partial(lax.all_to_all, axis_name=AXES, split_axis=0, concat_axis=0, tiled=True)
    done = smooth(swap(summed), block, size_x, size_y, tables)
    return turn_back(swap(done), block)


def solution(mesh):
    return jax.shard_map(
        body,
        mesh=mesh,
        in_specs=(P(None, None, "gx", "gy", None), P()),
        out_specs=P(None, "gx", "gy", None),
        check_vma=False,
    )
```

time: 169 us -> 145 us (0.86)
  blocking collectives: 58.8 us -> 122 us
  waiting for transfers between devices: 48.7 us -> 0 us
  Pallas kernels: 44 us -> 21.8 us
  starting transfers between devices: 11.9 us -> 0 us
  other arithmetic: 3.2 us -> 0 us
    all_to_all x1 -> x2, blocking collectives: 58.8 us -> 122 us  [the longest x1 64.6 us: body(): done = smooth(swap(summed), block, size_x, size_y, tables)]
    all_to_all x1 -> x0, waiting for transfers between devices: 48.7 us -> none  [body(): lax.all_to_all(summed, AXES, split_axis=0, concat_axis=0, tiled=True)]
    pallas_call x2, Pallas kernels: 27.1 us -> 12.2 us  [the longest x1 7.01 us: event_sum(): pl.pallas_call(functools.partial(sum_kernel, nx), in_specs=[pl.BlockSpec(...]
    all_to_all x1 -> x0, starting transfers between devices: 11.9 us -> none  [body(): lax.all_to_all(summed, AXES, split_axis=0, concat_axis=0, tiled=True)]
    pallas_call x1, Pallas kernels: 17 us -> 9.58 us  [smooth(): pl.pallas_call(functools.partial(smooth_kernel, size_y, block), grid=(par...]
    convert_element_type x3 -> x0, other arithmetic: 1.97 us -> none  [the longest x2 1.96 us: gauss_weights(): jnp.where(jnp.abs(offsets) <= radius, weights, 0.0).astype(jnp.bfloat16)]
  transfers between devices with their start and end apart: 1 -> 0, of which waited for: 1 -> 0; matrix products, arithmetic and copies ran while one was open for 3% -> 0% of each run, Pallas kernels for 0% -> 0%
where the time goes in v2:
time: 145 us
  blocking collectives  122 us (84%)
  Pallas kernels  21.8 us (15%)
    all_to_all x1, blocking collectives, body(): done = smooth(swap(summed), block, size_x, size_y, tables)  64.6 us
    all_to_all x1, blocking collectives, body(): return turn_back(swap(done), block)  57.7 us
    pallas_call x1, Pallas kernels, smooth(): pl.pallas_call(functools.partial(smooth_kernel, size_y, block), grid=(par...  9.58 us
    pallas_call x1, Pallas kernels, event_sum(): pl.pallas_call(functools.partial(sum_kernel, nx), in_specs=[pl.BlockSpec(...  7.01 us
    pallas_call x1, Pallas kernels, turn_back(): pl.pallas_call(turn_kernel, in_specs=[pl.BlockSpec(memory_space=pltpu.VME...  5.17 us

profile of v2, /device:TPU:1, one launch (start us, length us, event | category | flops | bytes accessed | tf_op | source)
XLA Modules:
  0.0 144.8 jit_solution(14274552139374389317)
XLA Ops:
  0.0 0.0 copy-start
  0.0 0.7 copy-done
  0.7 7.0 %event_sum.1 = (bf16[128,4,32,128]{3,2,1,0:T(8,128)(2,1)S(1)}, bf16[256,640]{1,0:T(8,128)(2,1)S(1)}, bf16[640,256]{1,0:T(8,128)(2,1)S(1)}, f32[1024,128]{1,0:T(8,128)S(1)}, f32[8,512]{1,0:T(8,128)S(1)}) custom-call(f32[4]{0:T(128)S(1)} %copy-done, bf16[4,4,2,32,64,128]{5,4,3,2,1,0:T(8,128)(2,1)} %bitcast.2), custom_call_target="tpu_custom_call" | custom-call | tf_op jit(solution)/shard_map/event_sum/pallas_call | solution.py:86
  7.7 64.6 %all_to_all.10.in_ref = bf16[128,4,32,128]{3,2,1,0:T(8,128)(2,1)S(1)} all-to-all(bf16[128,4,32,128]{3,2,1,0:T(8,128)(2,1)S(1)} %get-tuple-element.10), channel_id=1, replica_groups=mesh['gx'=16,'gy'=8] {'gx','gy'}, dimensions={0} | all-to-all | bytes 8388608 | tf_op jit(solution)/shard_map/all_to_all | solution.py:210
  72.3 9.6 %smooth.1 = bf16[128,4,32,128]{3,2,1,0:T(8,128)(2,1)S(1)} custom-call(bf16[128,4,32,128]{3,2,1,0:T(8,128)(2,1)S(1)} %all_to_all.10.in_ref, bf16[256,640]{1,0:T(8,128)(2,1)S(1)} %get-tuple-element.11.tile_ref, bf16[640,256]{1,0:T(8,128)(2,1)S(1)} %get-tuple-element.12.tile_t_ref, f32[1024,128]{1,0:T(8,128)S(1)} %get-tuple-element.13.inv_x_ref, ...), custom_call_target="tpu_custom_call" | custom-call | tf_op jit(solution)/shard_map/smooth/pallas_call | solution.py:149
  81.9 57.7 %all_to_all.11.in_ref = bf16[128,4,32,128]{3,2,1,0:T(8,128)(2,1)S(1)} all-to-all(bf16[128,4,32,128]{3,2,1,0:T(8,128)(2,1)S(1)} %smooth.1), channel_id=1, replica_groups=mesh['gx'=16,'gy'=8] {'gx','gy'}, dimensions={0} | all-to-all | bytes 8388608 | tf_op jit(solution)/shard_map/all_to_all | solution.py:211
  139.6 5.2 %turn_back.1 = f32[4,2,32,64,128]{4,3,2,1,0:T(8,128)} custom-call(bf16[128,4,32,128]{3,2,1,0:T(8,128)(2,1)S(1)} %all_to_all.11.in_ref), custom_call_target="tpu_custom_call" | custom-call | tf_op jit(solution)/shard_map/turn_back/pallas_call | solution.py:189
Async XLA Ops:
  0.0 0.7 copy-start

commit v3 on v2

v3 whole, which is shorter than its diff:
```python
import functools
import jax
import jax.numpy as jnp
from jax import lax
from jax.experimental import pallas as pl
from jax.experimental.pallas import tpu as pltpu
from jax.sharding import PartitionSpec as P

REACH = 3
MARGIN = 4
AXES = ("gx", "gy")
TILE = 8
SUM_MIB = 36
SMOOTH_MIB = 24
PLANES = 4
SUM_UNROLL = 2
TURN_UNROLL = 4
ROWS = 8


def gauss_weights(offsets, radius, sigma):
    values = offsets.astype(jnp.float32)
    weights = jnp.exp(-values * values / (2.0 * sigma * sigma))
    return jnp.where(jnp.abs(offsets) <= radius, weights, 0.0).astype(jnp.bfloat16)


def band(rows, cols, shift, axis, sigma, radius):
    far = lax.broadcasted_iota(jnp.int32, (rows, cols), axis)
    near = lax.broadcasted_iota(jnp.int32, (rows, cols), 1 - axis)
    return gauss_weights(far - near - shift, radius, sigma)


def clipped(first, window, margin, total):
    return max(0, margin - first), min(window, total - first + margin)


def make_tables(block, tile_ref, tile_t_ref, inv_x_ref, inv_y_ref):
    radius, sigma, margin = REACH * block, 2.0 * block, MARGIN * block
    step = 2 * block
    window = step + 2 * margin
    weights = band(step, window, margin, 1, sigma, radius)
    weights_t = band(window, step, margin, 0, sigma, radius)
    tile, reach = tile_ref.shape
    for at in range(0, tile, step):
        own = slice(at, at + step)
        tile_ref[own, at : at + window] = weights
        tile_t_ref[at : at + window, own] = weights_t
        for lo, hi in ((0, at), (at + window, reach)):
            if hi > lo:
                tile_ref[own, lo:hi] = jnp.zeros((step, hi - lo), tile_ref.dtype)
                tile_t_ref[lo:hi, own] = jnp.zeros((hi - lo, step), tile_t_ref.dtype)
    nx, ny = inv_x_ref.shape[0], inv_y_ref.shape[1]
    wide, wide_t = weights.astype(jnp.float32), weights_t.astype(jnp.float32)
    for x0 in range(0, nx, step):
        lo, hi = clipped(x0, window, margin, nx)
        sums = jnp.sum(wide[:, lo:hi], axis=1, keepdims=True)
        inv_x_ref[x0 : x0 + step] = jnp.broadcast_to(1.0 / sums, (step, inv_x_ref.shape[1]))
    for y0 in range(0, ny, step):
        lo, hi = clipped(y0, window, margin, ny)
        sums = jnp.sum(wide_t[lo:hi], axis=0, keepdims=True)
        inv_y_ref[:, y0 : y0 + step] = jnp.broadcast_to(1.0 / sums, (inv_y_ref.shape[0], step))


def sum_kernel(block, weight_hbm, kernels_ref, out_ref, *refs):
    tables, (landing, weight_ref, turned, arrived, weighed) = refs[:4], refs[4:]
    steps, events, halves, rows, width, depth = landing.shape
    per_param = steps // kernels_ref.shape[1]

    def copy(s):
        p, r = s // per_param, lax.rem(s, per_param)
        return pltpu.make_async_copy(
            kernels_ref.at[:, p, :, pl.ds(r * rows, rows)], landing.at[s], arrived.at[s]
        )

    weigh = pltpu.make_async_copy(weight_hbm, weight_ref, weighed)
    weigh.start()

    @pl.loop(0, steps)
    def _(s):
        copy(s).start()

    make_tables(block, *tables)
    weigh.wait()
    weight = [weight_ref[e] for e in range(events)]

    @pl.loop(0, steps, step=SUM_UNROLL)
    def _(first):
        for u in range(SUM_UNROLL):
            s = first + u
            copy(s).wait()
            for r in range(rows):
                parts = []
                for h in range(halves):
                    total = weight[0] * landing[s, 0, h, r].astype(jnp.float32)
                    for e in range(1, events):
                        total = total + weight[e] * landing[s, e, h, r].astype(jnp.float32)
                    parts.append(total)
                turned[u, pl.ds(r, depth, stride=rows), :] = jnp.concatenate(parts, axis=0).T
            p, place = s // per_param, pl.multiple_of(lax.rem(s, per_param) * rows, rows)
            whole = turned[u].reshape(depth, rows, halves * width)
            out_ref[:, p, pl.ds(place, rows)] = whole.astype(out_ref.dtype)


def event_sum(kernels, event_weight, nx_all, ny_all):
    events, params, nx, ny, depth = kernels.shape
    halves = depth // ny
    rows = nx // halves
    split = kernels.reshape(events, params, halves, rows, ny, depth)
    tile, reach = TILE * nx, (TILE + 2 * MARGIN) * nx
    steps = params * rows // ROWS
    vmem = pl.BlockSpec(memory_space=pltpu.VMEM)
    hbm = pl.BlockSpec(memory_space=pltpu.HBM)
    return pl.pallas_call(
        functools.partial(sum_kernel, nx),
        in_specs=[hbm, hbm],
        out_specs=(vmem,) * 5,
        out_shape=(
            jax.ShapeDtypeStruct((depth, params, rows, halves * ny), jnp.bfloat16),
            jax.ShapeDtypeStruct((tile, reach), jnp.bfloat16),
            jax.ShapeDtypeStruct((reach, tile), jnp.bfloat16),
            jax.ShapeDtypeStruct((nx_all, depth), jnp.float32),
            jax.ShapeDtypeStruct((8, ny_all), jnp.float32),
        ),
        scratch_shapes=[
            pltpu.VMEM((steps, events, halves, ROWS, ny, depth), jnp.bfloat16),
            pltpu.SMEM((events,), jnp.float32),
            pltpu.VMEM((SUM_UNROLL, depth * ROWS, halves * ny), jnp.float32),
            pltpu.SemaphoreType.DMA((steps,)),
            pltpu.SemaphoreType.DMA,
        ],
        compiler_params=pltpu.CompilerParams(vmem_limit_bytes=SUM_MIB << 20),
        name="event_sum",
    )(pltpu.with_memory_space_constraint(event_weight, pltpu.HBM), split)


def smooth_kernel(size_y, block, in_ref, tile_ref, tile_t_ref, inv_x_ref, inv_y_ref, out_ref, plane):
    _, pairs, nx, pair = plane.shape
    ny = pairs * pair
    rows = in_ref.shape[2]
    tile, reach = tile_ref.shape[0], MARGIN * block
    swap_halves = lambda a, b: (
        jnp.concatenate([a[:, :block], b[:, :block]], axis=1),
        jnp.concatenate([a[:, block:], b[:, block:]], axis=1),
    )

    def build(p, i):
        for j in range(pairs):
            at = i * size_y + 2 * j
            upper, lower = swap_halves(in_ref[at, p], in_ref[at + 1, p])
            plane[p, j, i * block : i * block + rows] = upper
            plane[p, j, i * block + rows : (i + 1) * block] = lower

    def build_for(p, x0):
        first = 0 if x0 == 0 else min(nx, x0 + reach) // block
        for i in range(first, min(nx, x0 + tile + reach) // block):
            build(p, i)

    def pack(p, x0, done):
        for i in range(tile // block):
            for j in range(0, size_y, 2):
                part = done[i * block : (i + 1) * block, j * block : j * block + pair]
                at = (x0 // block + i) * size_y + j
                out_ref[at, p], out_ref[at + 1, p] = swap_halves(part[:rows], part[rows:])

    jobs = [(p, x0) for p in range(in_ref.shape[1]) for x0 in range(0, nx, tile)]
    build_for(*jobs[0])
    last = None
    for k, (p, x0) in enumerate(jobs):
        lo, hi = max(0, x0 - reach), min(nx, x0 + tile + reach)
        at = lo - (x0 - reach)
        lines = jnp.concatenate([plane[p, j, lo:hi] for j in range(pairs)], axis=1)
        sums = jnp.dot(tile_ref[:, at : at + hi - lo], lines, preferred_element_type=jnp.float32)
        if k + 1 < len(jobs):
            build_for(*jobs[k + 1])
        inv_x = jnp.concatenate([inv_x_ref[x0 : x0 + tile]] * (ny // inv_x_ref.shape[1]), axis=1)
        along_x = (sums * inv_x).astype(jnp.bfloat16)
        if last is not None:
            pack(*last)
        parts = []
        for y0 in range(0, ny, tile):
            lo, hi = max(0, y0 - reach), min(ny, y0 + tile + reach)
            at = lo - (y0 - reach)
            sums = jnp.dot(along_x[:, lo:hi], tile_t_ref[at : at + hi - lo], preferred_element_type=jnp.float32)
            parts.append((sums * inv_y_ref[0:1, y0 : y0 + tile]).astype(jnp.bfloat16))
        last = p, x0, jnp.concatenate(parts, axis=1)
    pack(*last)


def smooth(lines, block, size_x, size_y, tables):
    blocks, params, rows, width = lines.shape
    nx = size_x * block
    whole = lambda a: pl.BlockSpec(a.shape, lambda p: (0,) * a.ndim)
    spec = pl.BlockSpec((blocks, PLANES, rows, width), lambda p: (0, p, 0, 0))
    return pl.pallas_call(
        functools.partial(smooth_kernel, size_y, block),
        grid=(params // PLANES,),
        in_specs=[spec] + [whole(t) for t in tables],
        out_specs=spec,
        out_shape=jax.ShapeDtypeStruct(lines.shape, jnp.bfloat16),
        scratch_shapes=[pltpu.VMEM((PLANES, size_y // 2, nx, 2 * block), jnp.bfloat16)],
        compiler_params=pltpu.CompilerParams(vmem_limit_bytes=SMOOTH_MIB << 20),
        name="smooth",
    )(lines, *tables)


def turn_kernel(in_ref, out_ref, leaving, wide, left):
    steps, halves, rows, width, _ = leaving.shape
    depth, params, _, pair = in_ref.shape
    per_param = steps // params

    def copy(s):
        p, r = s // per_param, lax.rem(s, per_param)
        return pltpu.make_async_copy(leaving.at[s], out_ref.at[p, :, pl.ds(r * rows, rows)], left.at[s])

    @pl.loop(0, steps, step=TURN_UNROLL)
    def _(first):
        for u in range(TURN_UNROLL):
            s = first + u
            p, place = s // per_param, pl.multiple_of(lax.rem(s, per_param) * rows, rows)
            wide[u] = in_ref[:, p, pl.ds(place, rows)].astype(jnp.float32).reshape(depth * rows, pair)
            for r in range(rows):
                turned = wide[u, pl.ds(r, depth, stride=rows), :].T
                for h in range(halves):
                    leaving[s, h, r] = turned[h * width : (h + 1) * width]
            copy(s).start()

    @pl.loop(0, steps)
    def _(s):
        copy(s).wait()


def turn_back(done, block):
    depth, params, rows, pair = done.shape
    halves = pair // block
    steps = params * rows // ROWS
    out = pl.pallas_call(
        turn_kernel,
        in_specs=[pl.BlockSpec(memory_space=pltpu.VMEM)],
        out_specs=pl.BlockSpec(memory_space=pl.ANY),
        out_shape=jax.ShapeDtypeStruct((params, halves, rows, block, depth), jnp.float32),
        scratch_shapes=[
            pltpu.VMEM((steps, halves, ROWS, block, depth), jnp.float32),
            pltpu.VMEM((TURN_UNROLL, depth * ROWS, pair), jnp.float32),
            pltpu.SemaphoreType.DMA((steps,)),
        ],
        compiler_params=pltpu.CompilerParams(vmem_limit_bytes=24 << 20),
        name="turn_back",
    )(done)
    return out.reshape(params, halves * rows, block, depth)


def body(kernels, event_weight):
    block = kernels.shape[2]
    size_x, size_y = lax.axis_size("gx"), lax.axis_size("gy")
    summed, *tables = event_sum(kernels, event_weight, size_x * block, size_y * block)
    swap = functools.partial(lax.all_to_all, axis_name=AXES, split_axis=0, concat_axis=0, tiled=True)
    done = smooth(swap(summed), block, size_x, size_y, tables)
    return turn_back(swap(done), block)


def solution(mesh):
    return jax.shard_map(
        body,
        mesh=mesh,
        in_specs=(P(None, None, "gx", "gy", None), P()),
        out_specs=P(None, "gx", "gy", None),
        check_vma=False,
    )
```

time: 145 us -> 139 us (0.959)
  Pallas kernels: 21.8 us -> 16.3 us
    pallas_call x1, Pallas kernels: 9.58 us -> 5.88 us  [smooth(): pl.pallas_call(functools.partial(smooth_kernel, size_y, block), grid=(par...]
where the time goes in v3:
time: 139 us
  blocking collectives  122 us (88%)
  Pallas kernels  16.3 us (12%)
    all_to_all x1, blocking collectives, body(): done = smooth(swap(summed), block, size_x, size_y, tables)  64.6 us
    all_to_all x1, blocking collectives, body(): return turn_back(swap(done), block)  57.7 us
    pallas_call x1, Pallas kernels, event_sum(): pl.pallas_call(functools.partial(sum_kernel, nx), in_specs=[hbm, hbm], ou...  6.41 us
    pallas_call x1, Pallas kernels, smooth(): pl.pallas_call(functools.partial(smooth_kernel, size_y, block), grid=(par...  5.88 us
    pallas_call x1, Pallas kernels, turn_back(): pl.pallas_call(turn_kernel, in_specs=[pl.BlockSpec(memory_space=pltpu.VME...  4.06 us

profile of v3, /device:TPU:1, one launch (start us, length us, event | category | flops | bytes accessed | tf_op | source)
XLA Modules:
  0.0 138.7 jit_solution(6172691189794084848)
XLA Ops:
  0.0 6.4 %event_sum.1 = (bf16[128,4,32,128]{3,2,1,0:T(8,128)(2,1)S(1)}, bf16[512,1024]{1,0:T(8,128)(2,1)S(1)}, bf16[1024,512]{1,0:T(8,128)(2,1)S(1)}, f32[1024,128]{1,0:T(8,128)S(1)}, f32[8,512]{1,0:T(8,128)S(1)}) custom-call(f32[4]{0:T(128)} %weight_hbm.1, bf16[4,4,2,32,64,128]{5,4,3,2,1,0:T(8,128)(2,1)} %bitcast.2), custom_call_target="tpu_custom_call" | custom-call | tf_op jit(solution)/shard_map/event_sum/pallas_call | solution.py:113
  6.4 64.6 %all_to_all.10.in_ref = bf16[128,4,32,128]{3,2,1,0:T(8,128)(2,1)S(1)} all-to-all(bf16[128,4,32,128]{3,2,1,0:T(8,128)(2,1)S(1)} %get-tuple-element.10), channel_id=1, replica_groups=mesh['gx'=16,'gy'=8] {'gx','gy'}, dimensions={0} | all-to-all | bytes 8388608 | tf_op jit(solution)/shard_map/all_to_all | solution.py:257
  71.0 5.9 %smooth.1 = bf16[128,4,32,128]{3,2,1,0:T(8,128)(2,1)S(1)} custom-call(bf16[128,4,32,128]{3,2,1,0:T(8,128)(2,1)S(1)} %all_to_all.10.in_ref, bf16[512,1024]{1,0:T(8,128)(2,1)S(1)} %get-tuple-element.11.tile_ref, bf16[1024,512]{1,0:T(8,128)(2,1)S(1)} %get-tuple-element.12.tile_t_ref, f32[1024,128]{1,0:T(8,128)S(1)} %get-tuple-element.13.inv_x_ref, ...), custom_call_target="tpu_custom_call" | custom-call | tf_op jit(solution)/shard_map/smooth/pallas_call | solution.py:194
  76.9 57.7 %all_to_all.11.in_ref = bf16[128,4,32,128]{3,2,1,0:T(8,128)(2,1)S(1)} all-to-all(bf16[128,4,32,128]{3,2,1,0:T(8,128)(2,1)S(1)} %smooth.1), channel_id=1, replica_groups=mesh['gx'=16,'gy'=8] {'gx','gy'}, dimensions={0} | all-to-all | bytes 8388608 | tf_op jit(solution)/shard_map/all_to_all | solution.py:258
  134.6 4.1 %turn_back.1 = f32[4,2,32,64,128]{4,3,2,1,0:T(8,128)} custom-call(bf16[128,4,32,128]{3,2,1,0:T(8,128)(2,1)S(1)} %all_to_all.11.in_ref), custom_call_target="tpu_custom_call" | custom-call | tf_op jit(solution)/shard_map/turn_back/pallas_call | solution.py:236

commit v4 on v3

--- a/solution.py
+++ b/solution.py
@@ -10,11 +10,12 @@
 MARGIN = 4
 AXES = ("gx", "gy")
 TILE = 8
+X_TILES = (5, 6, 5)
 SUM_MIB = 36
 SMOOTH_MIB = 24
 PLANES = 4
 SUM_UNROLL = 2
-TURN_UNROLL = 4
+TURN_UNROLL = 16
 ROWS = 8
 
 
@@ -137,7 +138,7 @@
     _, pairs, nx, pair = plane.shape
     ny = pairs * pair
     rows = in_ref.shape[2]
-    tile, reach = tile_ref.shape[0], MARGIN * block
+    tile, margin = tile_ref.shape[0], MARGIN * block
     swap_halves = lambda a, b: (
         jnp.concatenate([a[:, :block], b[:, :block]], axis=1),
         jnp.concatenate([a[:, block:], b[:, block:]], axis=1),
@@ -150,40 +151,58 @@
             plane[p, j, i * block : i * block + rows] = upper
             plane[p, j, i * block + rows : (i + 1) * block] = lower
 
-    def build_for(p, x0):
-        first = 0 if x0 == 0 else min(nx, x0 + reach) // block
-        for i in range(first, min(nx, x0 + tile + reach) // block):
-            build(p, i)
+    def window(x0, x1):
+        return max(0, x0 - REACH * block) // pair * pair, min(nx, -(-(x1 + REACH * block) // pair) * pair)
 
     def pack(p, x0, done):
-        for i in range(tile // block):
+        for i in range(done.shape[0] // block):
             for j in range(0, size_y, 2):
                 part = done[i * block : (i + 1) * block, j * block : j * block + pair]
                 at = (x0 // block + i) * size_y + j
                 out_ref[at, p], out_ref[at + 1, p] = swap_halves(part[:rows], part[rows:])
 
-    jobs = [(p, x0) for p in range(in_ref.shape[1]) for x0 in range(0, nx, tile)]
-    build_for(*jobs[0])
-    last = None
-    for k, (p, x0) in enumerate(jobs):
-        lo, hi = max(0, x0 - reach), min(nx, x0 + tile + reach)
-        at = lo - (x0 - reach)
+    ends = [block * sum(X_TILES[:k]) for k in range(len(X_TILES) + 1)]
+    assert ends[-1] == nx
+    built = dict.fromkeys(range(in_ref.shape[1]), 0)
+
+    def build_for(p, x0, x1):
+        while built[p] * block < window(x0, x1)[1]:
+            build(p, built[p])
+            built[p] += 1
+
+    def along_x(p, x0, x1):
+        lo, hi = window(x0, x1)
+        row = (x0 - lo) % pair
+        col = margin + lo - x0 + row
         lines = jnp.concatenate([plane[p, j, lo:hi] for j in range(pairs)], axis=1)
-        sums = jnp.dot(tile_ref[:, at : at + hi - lo], lines, preferred_element_type=jnp.float32)
-        if k + 1 < len(jobs):
-            build_for(*jobs[k + 1])
-        inv_x = jnp.concatenate([inv_x_ref[x0 : x0 + tile]] * (ny // inv_x_ref.shape[1]), axis=1)
-        along_x = (sums * inv_x).astype(jnp.bfloat16)
-        if last is not None:
-            pack(*last)
+        weights = tile_ref[row : row + x1 - x0, col : col + hi - lo]
+        sums = jnp.dot(weights, lines, preferred_element_type=jnp.float32)
+        inv_x = jnp.concatenate([inv_x_ref[x0:x1]] * (ny // inv_x_ref.shape[1]), axis=1)
+        return (sums * inv_x).astype(jnp.bfloat16)
+
+    def along_y(rows_in):
         parts = []
         for y0 in range(0, ny, tile):
-            lo, hi = max(0, y0 - reach), min(ny, y0 + tile + reach)
-            at = lo - (y0 - reach)
-            sums = jnp.dot(along_x[:, lo:hi], tile_t_ref[at : at + hi - lo], preferred_element_type=jnp.float32)
+            lo, hi = max(0, y0 - margin), min(ny, y0 + tile + margin)
+            at = lo - (y0 - margin)
+            sums = jnp.dot(rows_in[:, lo:hi], tile_t_ref[at : at + hi - lo], preferred_element_type=jnp.float32)
             parts.append((sums * inv_y_ref[0:1, y0 : y0 + tile]).astype(jnp.bfloat16))
-        last = p, x0, jnp.concatenate(parts, axis=1)
-    pack(*last)
+        return jnp.concatenate(parts, axis=1)
+
+    tiles = list(zip(ends, ends[1:]))
+    params = in_ref.shape[1]
+    for x0, x1 in tiles:
+        build_for(0, x0, x1)
+    last = None
+    for p in range(params):
+        mixed = jnp.concatenate([along_x(p, x0, x1) for x0, x1 in tiles], axis=0)
+        if p + 1 < params:
+            for x0, x1 in tiles:
+                build_for(p + 1, x0, x1)
+        if last is not None:
+            pack(p - 1, 0, last)
+        last = along_y(mixed)
+    pack(params - 1, 0, last)
 
 
 def smooth(lines, block, size_x, size_y, tables):

time: 139 us -> 138 us (level)
  no operation moved by 1% of the time
where the time goes in v4:
time: 138 us
  blocking collectives  122 us (88%)
  Pallas kernels  15.3 us (11%)
    all_to_all x1, blocking collectives, body(): done = smooth(swap(summed), block, size_x, size_y, tables)  64.6 us
    all_to_all x1, blocking collectives, body(): return turn_back(swap(done), block)  57.7 us
    pallas_call x1, Pallas kernels, event_sum(): pl.pallas_call(functools.partial(sum_kernel, nx), in_specs=[hbm, hbm], ou...  6.41 us
    pallas_call x1, Pallas kernels, smooth(): pl.pallas_call(functools.partial(smooth_kernel, size_y, block), grid=(par...  5.2 us
    pallas_call x1, Pallas kernels, turn_back(): pl.pallas_call(turn_kernel, in_specs=[pl.BlockSpec(memory_space=pltpu.VME...  3.71 us

profile of v4, /device:TPU:1, one launch (start us, length us, event | category | flops | bytes accessed | tf_op | source)
XLA Modules:
  0.0 137.7 jit_solution(14750188650134099242)
XLA Ops:
  0.0 6.4 %event_sum.1 = (bf16[128,4,32,128]{3,2,1,0:T(8,128)(2,1)S(1)}, bf16[512,1024]{1,0:T(8,128)(2,1)S(1)}, bf16[1024,512]{1,0:T(8,128)(2,1)S(1)}, f32[1024,128]{1,0:T(8,128)S(1)}, f32[8,512]{1,0:T(8,128)S(1)}) custom-call(f32[4]{0:T(128)} %weight_hbm.1, bf16[4,4,2,32,64,128]{5,4,3,2,1,0:T(8,128)(2,1)} %bitcast.2), custom_call_target="tpu_custom_call" | custom-call | tf_op jit(solution)/shard_map/event_sum/pallas_call | solution.py:114
  6.4 64.6 %all_to_all.10.in_ref = bf16[128,4,32,128]{3,2,1,0:T(8,128)(2,1)S(1)} all-to-all(bf16[128,4,32,128]{3,2,1,0:T(8,128)(2,1)S(1)} %get-tuple-element.10), channel_id=1, replica_groups=mesh['gx'=16,'gy'=8] {'gx','gy'}, dimensions={0} | all-to-all | bytes 8388608 | tf_op jit(solution)/shard_map/all_to_all | solution.py:276
  71.0 5.2 %smooth.1 = bf16[128,4,32,128]{3,2,1,0:T(8,128)(2,1)S(1)} custom-call(bf16[128,4,32,128]{3,2,1,0:T(8,128)(2,1)S(1)} %all_to_all.10.in_ref, bf16[512,1024]{1,0:T(8,128)(2,1)S(1)} %get-tuple-element.11.tile_ref, bf16[1024,512]{1,0:T(8,128)(2,1)S(1)} %get-tuple-element.12.tile_t_ref, f32[1024,128]{1,0:T(8,128)S(1)} %get-tuple-element.13.inv_x_ref, ...), custom_call_target="tpu_custom_call" | custom-call | tf_op jit(solution)/shard_map/smooth/pallas_call | solution.py:213
  76.2 57.7 %all_to_all.11.in_ref = bf16[128,4,32,128]{3,2,1,0:T(8,128)(2,1)S(1)} all-to-all(bf16[128,4,32,128]{3,2,1,0:T(8,128)(2,1)S(1)} %smooth.1), channel_id=1, replica_groups=mesh['gx'=16,'gy'=8] {'gx','gy'}, dimensions={0} | all-to-all | bytes 8388608 | tf_op jit(solution)/shard_map/all_to_all | solution.py:277
  133.9 3.7 %turn_back.1 = f32[4,2,32,64,128]{4,3,2,1,0:T(8,128)} custom-call(bf16[128,4,32,128]{3,2,1,0:T(8,128)(2,1)S(1)} %all_to_all.11.in_ref), custom_call_target="tpu_custom_call" | custom-call | tf_op jit(solution)/shard_map/turn_back/pallas_call | solution.py:255

commit v5 on v4

--- a/solution.py
+++ b/solution.py
@@ -13,6 +13,7 @@
 X_TILES = (5, 6, 5)
 SUM_MIB = 36
 SMOOTH_MIB = 24
+LAST_PARTS = 2
 PLANES = 4
 SUM_UNROLL = 2
 TURN_UNROLL = 16
@@ -191,18 +192,28 @@
 
     tiles = list(zip(ends, ends[1:]))
     params = in_ref.shape[1]
-    for x0, x1 in tiles:
-        build_for(0, x0, x1)
     last = None
     for p in range(params):
-        mixed = jnp.concatenate([along_x(p, x0, x1) for x0, x1 in tiles], axis=0)
+        mixed = []
+        for x0, x1 in tiles:
+            build_for(p, x0, x1)
+            mixed.append(along_x(p, x0, x1))
+        mixed = jnp.concatenate(mixed, axis=0)
         if p + 1 < params:
             for x0, x1 in tiles:
                 build_for(p + 1, x0, x1)
         if last is not None:
             pack(p - 1, 0, last)
-        last = along_y(mixed)
-    pack(params - 1, 0, last)
+        if p + 1 < params:
+            last = along_y(mixed)
+    part = nx // LAST_PARTS
+    ready = None
+    for x0 in range(0, nx, part):
+        done = along_y(mixed[x0 : x0 + part])
+        if ready is not None:
+            pack(params - 1, x0 - part, ready)
+        ready = done
+    pack(params - 1, nx - part, ready)
 
 
 def smooth(lines, block, size_x, size_y, tables):
@@ -241,7 +252,7 @@
                 turned = wide[u, pl.ds(r, depth, stride=rows), :].T
                 for h in range(halves):
                     leaving[s, h, r] = turned[h * width : (h + 1) * width]
-            copy(s).start()
+            copy(s).start(priority=u % 2)
 
     @pl.loop(0, steps)
     def _(s):

time: 138 us -> 138 us (level)
  no operation moved by 1% of the time
where the time goes in v5:
time: 138 us
  blocking collectives  122 us (88%)
  Pallas kernels  15.3 us (11%)
    all_to_all x1, blocking collectives, body(): done = smooth(swap(summed), block, size_x, size_y, tables)  64.6 us
    all_to_all x1, blocking collectives, body(): return turn_back(swap(done), block)  57.7 us
    pallas_call x1, Pallas kernels, event_sum(): pl.pallas_call(functools.partial(sum_kernel, nx), in_specs=[hbm, hbm], ou...  6.41 us
    pallas_call x1, Pallas kernels, smooth(): pl.pallas_call(functools.partial(smooth_kernel, size_y, block), grid=(par...  5.2 us
    pallas_call x1, Pallas kernels, turn_back(): pl.pallas_call(turn_kernel, in_specs=[pl.BlockSpec(memory_space=pltpu.VME...  3.71 us

profile of v5, /device:TPU:1, one launch (start us, length us, event | category | flops | bytes accessed | tf_op | source)
XLA Modules:
  0.0 137.7 jit_solution(11313057952702038229)
XLA Ops:
  0.0 6.4 %event_sum.1 = (bf16[128,4,32,128]{3,2,1,0:T(8,128)(2,1)S(1)}, bf16[512,1024]{1,0:T(8,128)(2,1)S(1)}, bf16[1024,512]{1,0:T(8,128)(2,1)S(1)}, f32[1024,128]{1,0:T(8,128)S(1)}, f32[8,512]{1,0:T(8,128)S(1)}) custom-call(f32[4]{0:T(128)} %weight_hbm.1, bf16[4,4,2,32,64,128]{5,4,3,2,1,0:T(8,128)(2,1)} %bitcast.2), custom_call_target="tpu_custom_call" | custom-call | tf_op jit(solution)/shard_map/event_sum/pallas_call | solution.py:115
  6.4 64.6 %all_to_all.10.in_ref = bf16[128,4,32,128]{3,2,1,0:T(8,128)(2,1)S(1)} all-to-all(bf16[128,4,32,128]{3,2,1,0:T(8,128)(2,1)S(1)} %get-tuple-element.10), channel_id=1, replica_groups=mesh['gx'=16,'gy'=8] {'gx','gy'}, dimensions={0} | all-to-all | bytes 8388608 | tf_op jit(solution)/shard_map/all_to_all | solution.py:287
  71.0 5.2 %smooth.1 = bf16[128,4,32,128]{3,2,1,0:T(8,128)(2,1)S(1)} custom-call(bf16[128,4,32,128]{3,2,1,0:T(8,128)(2,1)S(1)} %all_to_all.10.in_ref, bf16[512,1024]{1,0:T(8,128)(2,1)S(1)} %get-tuple-element.11.tile_ref, bf16[1024,512]{1,0:T(8,128)(2,1)S(1)} %get-tuple-element.12.tile_t_ref, f32[1024,128]{1,0:T(8,128)S(1)} %get-tuple-element.13.inv_x_ref, ...), custom_call_target="tpu_custom_call" | custom-call | tf_op jit(solution)/shard_map/smooth/pallas_call | solution.py:224
  76.2 57.7 %all_to_all.11.in_ref = bf16[128,4,32,128]{3,2,1,0:T(8,128)(2,1)S(1)} all-to-all(bf16[128,4,32,128]{3,2,1,0:T(8,128)(2,1)S(1)} %smooth.1), channel_id=1, replica_groups=mesh['gx'=16,'gy'=8] {'gx','gy'}, dimensions={0} | all-to-all | bytes 8388608 | tf_op jit(solution)/shard_map/all_to_all | solution.py:288
  133.9 3.7 %turn_back.1 = f32[4,2,32,64,128]{4,3,2,1,0:T(8,128)} custom-call(bf16[128,4,32,128]{3,2,1,0:T(8,128)(2,1)S(1)} %all_to_all.11.in_ref), custom_call_target="tpu_custom_call" | custom-call | tf_op jit(solution)/shard_map/turn_back/pallas_call | solution.py:266
